TPU v7x, 256 devices: a whole 4x4x8 slice. The times are simulated.
256 devices in a mesh: dp: 32 (over x, z), tp: 8 (over y, core).
Axes of the slice: x: 4, y: 4, z: 8, core: 2. Of those that a mesh axis runs over, the one named last changes fastest.
Arguments:
- hidden_state: bfloat16 [7168, 512], P(None, 'dp'), may hold values from -6 to 6
- attention_gain: float32 [7168], replicated, may hold values from 0.1 to 1.9
- down_weight: bfloat16 [7168, 2112], P(None, 'tp'), may hold values from -0.0625 to 0.0625
- query_gain: float32 [1536], replicated, may hold values from 0.1 to 1.9
- latent_gain: float32 [512], replicated, may hold values from 0.1 to 1.9
- query_weight: bfloat16 [128, 576, 1536], P('tp', 'dp'), may hold values from -0.15625 to 0.15625
- latent_cache: bfloat16 [256, 4096, 576], P('dp'), may hold values from -240 to 240
- cache_length: int32 [256], P('dp'), may hold values from 1 to 4096
- owner_place: int32 [256], replicated, may hold values from 0 to 255, each once
- accept_length: int32 [256], replicated, may hold values from 1 to 2
- value_weight: bfloat16 [128, 512, 128], P('tp'), may hold values from -0.25 to 0.25
- output_weight: bfloat16 [7168, 16384], P('dp', 'tp'), may hold values from -0.046875 to 0.046875
- final_gain: float32 [7168], replicated, may hold values from 0.1 to 1.9
- head_weight: bfloat16 [7168, 65536], P(None, ('dp', 'tp')), may hold values from -8 to 8
- draft_tokens: int32 [256, 2], replicated, may hold values from 0 to 65535
Outputs:
- log_probs: float32 [512, 65536], P(None, ('dp', 'tp'))
- draft_scores: float32 [512], replicated
- committed: bfloat16 [256, 2, 576], P('dp')
All inputs are finite; a program needn't handle non-finite values.
Results may differ from a plain program's by a relative error of at most 0.006.
The roundings to bfloat16 on the way count: a program that leaves them out, or rounds other values in their place, can miss the bound.
Values may be sent and summed in bfloat16 or wider, within the bound.
No kernel may reach another device: no remote copies, remote signals or barrier semaphores. Data moves between devices by JAX's collectives and lax.ppermute only.
A program may use at most 192 MiB of HBM per device.

v0:
```python
import jax
import jax.numpy as jnp
from jax import lax
from jax.sharding import PartitionSpec as P

D = 7168
QL = 1536
DL = 512
DR = 64
epsilon = 1e-06
score_scale = 192.0 ** (-0.5)
masked_score = -1e30


def row_norm(values, gain_vector):
    inverse_rms = lax.rsqrt(jnp.mean(values * values, axis=-1, keepdims=True) + epsilon)
    return values * inverse_rms * gain_vector


def round_keep(values):
    return lax.optimization_barrier(values.astype(jnp.bfloat16)).astype(jnp.float32)


def on_device(
    hidden_state,
    attention_gain,
    down_weight,
    query_gain,
    latent_gain,
    query_weight,
    latent_cache,
    cache_length,
    owner_place,
    accept_length,
    value_weight,
    output_weight,
    final_gain,
    head_weight,
    draft_tokens,
):
    dp_count = lax.axis_size("dp")
    tp_count = lax.axis_size("tp")
    dp_rank = lax.axis_index("dp")
    tp_rank = lax.axis_index("tp")
    request_count = draft_tokens.shape[0]
    step_count = draft_tokens.shape[1]
    row_count = request_count * step_count
    local_requests = latent_cache.shape[0]
    local_rows = local_requests * step_count
    context = latent_cache.shape[1]
    slice_width = query_weight.shape[1]
    local_heads = value_weight.shape[0]
    value_width = value_weight.shape[2]
    stream = hidden_state.astype(jnp.float32)
    scaled = (stream * attention_gain[:, None]).astype(jnp.bfloat16)
    column_part = lax.dot_general(
        scaled, down_weight, (((0,), (0,)), ((), ())), preferred_element_type=jnp.float32
    )
    projected = lax.all_gather(column_part, "tp", axis=1, tiled=True)
    inverse_norm = lax.rsqrt(jnp.sum(stream * stream, axis=0) / D + epsilon)
    latent = projected * inverse_norm[:, None]
    query_latent = row_norm(latent[:, :QL], query_gain).astype(jnp.bfloat16)
    latent_part = row_norm(latent[:, QL : QL + DL], latent_gain)
    fresh_rows = jnp.concatenate([latent_part, latent[:, QL + DL :]], axis=1).astype(jnp.bfloat16)
    every_query, every_fresh = (
        lax.all_gather(query_latent, "dp", axis=0, tiled=True),
        lax.all_gather(fresh_rows, "dp", axis=0, tiled=True),
    )
    query_part = lax.dot_general(
        every_query, query_weight, (((1,), (2,)), ((), ())), preferred_element_type=jnp.float32
    )
    query_part = query_part.astype(jnp.bfloat16).reshape(row_count, local_heads * slice_width)
    step_index = jnp.arange(step_count, dtype=jnp.int32)
    owner_row = (owner_place[:, None] * step_count + step_index[None, :]).reshape(row_count)
    row_index = jnp.arange(row_count, dtype=jnp.int32)
    reorder = (owner_row[None, :] == row_index[:, None]).astype(jnp.bfloat16)
    query_owned = jnp.dot(reorder, query_part, preferred_element_type=jnp.float32).astype(
        jnp.bfloat16
    )
    own_reorder = lax.dynamic_slice_in_dim(reorder, dp_rank * local_rows, local_rows, 0)
    own_fresh = jnp.dot(own_reorder, every_fresh, preferred_element_type=jnp.float32).astype(
        jnp.bfloat16
    )
    own_fresh = own_fresh.reshape(local_requests, step_count, DL + DR)
    arrived = lax.all_to_all(query_owned, "dp", split_axis=0, concat_axis=1, tiled=True)
    arrived = arrived.reshape(local_requests, step_count, dp_count, local_heads, slice_width)
    cache_blocks = latent_cache.reshape(local_requests, context, dp_count, slice_width)
    fresh_blocks = own_fresh.reshape(local_requests, step_count, dp_count, slice_width)
    old_scores = (
        jnp.einsum("usdhc,updc->ushp", arrived, cache_blocks, preferred_element_type=jnp.float32)
        * score_scale
    )
    live_mask = jnp.arange(context, dtype=jnp.int32)[None, :] < cache_length[:, None]
    old_scores = jnp.where(live_mask[:, None, None, :], old_scores, masked_score)
    new_scores = (
        jnp.einsum("usdhc,ukdc->ushk", arrived, fresh_blocks, preferred_element_type=jnp.float32)
        * score_scale
    )
    causal = step_index[None, :] <= step_index[:, None]
    new_scores = jnp.where(causal[None, :, None, :], new_scores, masked_score)
    row_peak = jnp.maximum(jnp.max(old_scores, axis=-1), jnp.max(new_scores, axis=-1))
    old_exp = jnp.exp(old_scores - row_peak[..., None])
    new_exp = jnp.exp(new_scores - row_peak[..., None])
    exp_total = jnp.sum(old_exp, axis=-1) + jnp.sum(new_exp, axis=-1)
    old_weight = (old_exp / exp_total[..., None]).astype(jnp.bfloat16)
    new_weight = (new_exp / exp_total[..., None]).astype(jnp.bfloat16)
    mixed_values = jnp.einsum(
        "ushp,upc->ushc", old_weight, latent_cache[:, :, :DL], preferred_element_type=jnp.float32
    )
    mixed_values = mixed_values + jnp.einsum(
        "ushk,ukc->ushc", new_weight, own_fresh[:, :, :DL], preferred_element_type=jnp.float32
    )
    attended = mixed_values.astype(jnp.bfloat16)
    head_values = jnp.einsum(
        "ushc,hcv->ushv", attended, value_weight, preferred_element_type=jnp.float32
    )
    head_values = head_values.astype(jnp.bfloat16).reshape(local_rows, local_heads * value_width)
    slot_terms = lax.dot_general(
        output_weight,
        lax.all_gather(head_values, "dp", axis=0, tiled=True),
        (((1,), (1,)), ((), ())),
        preferred_element_type=jnp.float32,
    )
    request_terms = jnp.take(slot_terms, owner_row, axis=1)
    block_sum = lax.psum(request_terms, "tp")
    attn_output = lax.all_to_all(
        block_sum.astype(jnp.bfloat16), "dp", split_axis=1, concat_axis=0, tiled=True
    ).astype(block_sum.dtype)
    residual = round_keep(stream + attn_output)
    square_total = jnp.sum(residual * residual, axis=0)
    normed = residual * lax.rsqrt(square_total / D + epsilon)[None, :] * final_gain[:, None]
    normed = normed.astype(jnp.bfloat16)
    whole_normed = lax.all_gather(normed, "dp", axis=1, tiled=True)
    logits = lax.dot_general(
        whole_normed, head_weight, (((0,), (0,)), ((), ())), preferred_element_type=jnp.float32
    )
    vocab_width = head_weight.shape[1]
    vocab_start = (dp_rank * tp_count + tp_rank) * vocab_width
    draft_flat = draft_tokens.reshape(row_count)
    target_hit = (draft_flat - vocab_start)[:, None] == jnp.arange(vocab_width, dtype=jnp.int32)[
        None, :
    ]
    target_part = jnp.sum(jnp.where(target_hit, logits, jnp.zeros_like(logits)), axis=1)
    local_peak = jnp.max(logits, axis=1)
    vocab_peak = lax.pmax(local_peak, ("dp", "tp"))
    shifted_total = jnp.sum(jnp.exp(logits - vocab_peak[:, None]), axis=1)
    vocab_total, target = lax.psum((shifted_total, target_part), ("dp", "tp"))
    log_total = vocab_peak + jnp.log(vocab_total)
    accepted = (step_index[None, :] < accept_length[:, None]).reshape(row_count)
    log_probs = jnp.where(accepted[:, None], logits - log_total[:, None], jnp.zeros_like(logits))
    draft_scores = jnp.where(accepted, target - log_total, jnp.zeros_like(target))
    slot_global = dp_rank * local_requests + jnp.arange(local_requests, dtype=jnp.int32)
    slot_match = owner_place[None, :] == slot_global[:, None]
    slot_accept = jnp.sum(
        jnp.where(slot_match, accept_length[None, :], jnp.zeros_like(slot_match, dtype=jnp.int32)),
        axis=1,
    )
    keep_mask = step_index[None, :, None] < slot_accept[:, None, None]
    committed = jnp.where(keep_mask, own_fresh, jnp.zeros_like(own_fresh))
    return (log_probs, draft_scores, committed)


def solution(mesh):
    return jax.shard_map(
        on_device,
        mesh=mesh,
        in_specs=(
            P(None, "dp"),
            P(),
            P(None, "tp"),
            P(),
            P(),
            P("tp", "dp", None),
            P("dp", None, None),
            P("dp"),
            P(),
            P(),
            P("tp", None, None),
            P("dp", "tp"),
            P(),
            P(None, ("dp", "tp")),
            P(),
        ),
        out_specs=(P(None, ("dp", "tp")), P(), P("dp", None, None)),
        check_vma=False,
    )
```

profile of v0, /device:TPU:1, one launch (start us, length us, event | category | flops | bytes accessed | tf_op | source)
XLA Modules:
  0.0 611.3 jit_solution(11450530921332447881)
XLA Ops:
  7.3 1.2 fusion.38
  8.5 3.4 convolution_bitcast_fusion.1
  11.9 15.8 %all-gather = f32[8,264,16]{1,2,0:T(8,128)S(1)} all-gather(f32[1,264,16]{1,2,0:T(8,128)S(1)} %convolution_bitcast_fusion.1), channel_id=1, replica_groups=mesh['dp'=32,'tp'=8] {'tp'}, dimensions={0}, use_global_device_ids=true | all-gather | bytes 152064 | tf_op jit(solution)/shard_map/all_gather | solution.py:59
  28.1 0.7 multiply_convert_fusion
  29.4 40.8 %all_gather.17 = bf16[512,576]{1,0:T(8,128)(2,1)S(1)} all-gather(bf16[16,576]{1,0:T(8,128)(2,1)S(1)} %pad_maximum_fusion), channel_id=1, replica_groups=mesh['dp'=32,'tp'=8] {'dp'}, dimensions={0}, use_global_device_ids=true | all-gather | bytes 608256 | tf_op jit(solution)/shard_map/all_gather | solution.py:67
  71.1 32.7 %copy.58 = bf16[8,4096,576]{1,0,2:T(8,128)(2,1)} copy(bf16[8,4096,576]{1,2,0:T(8,128)(2,1)} %param.21) | data formatting | bytes 75497472 | tf_op args[6]
  103.9 2.5 fusion.19
  106.5 0.4 convolution_convert_fusion
  106.9 0.9 copy.56
  107.8 6.1 all-to-all-start
  114.1 10.1 %all-to-all-done = bf16[32,16,288]{2,1,0:T(8,128)(2,1)S(1)} async-done(((bf16[32,16,288]{2,1,0:T(8,128)(2,1)}), bf16[32,16,288]{2,1,0:T(8,128)(2,1)S(1)}, u32[]{:S(2)}, u32[]{:S(2)}) %all-to-all-start) | async-done | bytes 294944 | tf_op jit(solution)/shard_map/all_to_all | solution.py:85
  124.2 2.2 copy.57
  126.4 2.8 fusion.50
  129.2 73.5 %fusion.8 = (f32[8,2,16]{2,1,0:T(2,128)S(1)}, f32[8,2,16,4096]{3,2,1,0:T(8,128)S(1)}) fusion(pred[8,4096]{1,0:T(8,128)(4,1)S(1)} %iota_compare_fusion.2, bf16[8,4096,32,18,1]{1,0,3,2,4:T(8,128)(2,1)} %bitcast.77, bf16[8,2,32,16,18]{2,1,0,4,3:T(2,128)(2,1)} %bitcast.80), kind=kOutput, calls=%fused_computation.10 | convolution fusion | flops 1211105024 | bytes 42271744 | tf_op jit(solution)/shard_map/usdhc,updc->ushp/dot_general | solution.py:90
  202.7 1.9 copy-done.1
  204.6 1.2 fusion.9
  205.8 15.8 %fusion.2 = f32[8,2,16,512]{3,2,1,0:T(8,128)S(1)} fusion(bf16[8,4096,576]{1,2,0:T(8,128)(2,1)} %param.21, f32[8,2,16,4096]{3,2,1,0:T(8,128)} %copy-done.1, f32[8,2,16]{2,1,0:T(2,128)S(1)} %add.129, f32[8,2,16]{2,1,0:T(2,128)S(1)} %max.9, pred[8,4096]{1,0:T(8,128)(4,1)S(1)} %iota_compare_fusion.2), kind=kOutput, calls=%fused_computation.3 | convolution fusion | flops 1078984704 | bytes 38307840 | tf_op jit(solution)/shard_map/ushp,upc->ushc/dot_general | solution.py:107
  221.9 0.5 fusion.27
  222.3 0.6 copy.102
  223.2 81.2 %all-gather.7.cloned.1.call-done = bf16[512,2048]{1,0:T(8,128)(2,1)} async-done(((bf16[16,2048]{1,0:T(8,128)(2,1)}), bf16[512,2048]{1,0:T(8,128)(2,1)}) %all-gather.7.cloned.1.call-update) | async-done | bytes 2097168 | tf_op jit(solution)/shard_map/all_gather | solution.py:120
  304.5 2.6 convolution_bitcast_fusion
  307.3 1.6 gather_fusion
  309.1 30.8 %all-reduce.2 = bf16[224,512]{0,1:T(8,128)(2,1)S(1)} all-reduce(f32[224,512]{0,1:T(8,128)S(1)} %select_bitcast_fusion), channel_id=1, replica_groups=mesh['dp'=32,'tp'=8] {'tp'}, use_global_device_ids=true, to_apply=%region_7.8 | all-reduce | flops 114688 | bytes 688128 | tf_op jit(solution)/shard_map/psum | solution.py:125
  339.9 14.9 %all_to_all.29 = bf16[224,32,16]{0,2,1:T(8,128)(2,1)S(1)} all-to-all(bf16[224,32,16]{0,2,1:T(8,128)(2,1)S(1)} %bitcast.81), channel_id=1, replica_groups=mesh['dp'=32,'tp'=8] {'dp'}, dimensions={1} | all-to-all | bytes 458752 | tf_op jit(solution)/shard_map/all_to_all | solution.py:126
  355.8 0.8 fusion.36
  357.4 0.7 broadcast_select_fusion
  358.1 90.3 %all-gather.9.cloned.1.call-done = bf16[7168,512]{0,1:T(8,128)(2,1)} async-done(((bf16[7168,16]{0,1:T(8,128)(2,1)}), bf16[7168,512]{0,1:T(8,128)(2,1)}) %all-gather.9.cloned.1.call-update) | async-done | bytes 7340048 | tf_op jit(solution)/shard_map/all_gather | solution.py:133
  448.5 6.2 %fusion.51 = (f32[512]{0:T(512)S(1)}, f32[512,256]{0,1:T(8,128)S(1)}) fusion(bf16[7168,512]{0,1:T(8,128)(2,1)} %all-gather.9.cloned.1.call-done, bf16[7168,256]{1,0:T(8,128)(2,1)} %param.28), kind=kOutput, calls=%fused_computation.95 | convolution fusion | flops 1879178752 | bytes 11536384 | tf_op jit(solution)/shard_map/dot_general | solution.py:134
  454.7 75.1 %pmax.7 = f32[512]{0:T(512)S(1)} all-reduce(f32[512]{0:T(512)S(1)} %get-tuple-element.25), channel_id=1, replica_groups=mesh['dp'=32,'tp'=8] {'dp','tp'}, use_global_device_ids=true, to_apply=%region_10.11 | all-reduce | flops 512 | bytes 4096 | tf_op jit(solution)/shard_map/pmax | solution.py:145
  529.9 72.8 %all-reduce = (f32[512]{0:T(512)S(1)}, f32[512]{0:T(512)S(1)}) all-reduce(f32[512]{0:T(512)S(1)} %get-tuple-element.16, f32[512]{0:T(512)S(1)} %get-tuple-element.15), channel_id=1, replica_groups=mesh['dp'=32,'tp'=8] {'dp','tp'}, use_global_device_ids=true, to_apply=%region_12.13 | all-reduce | flops 1024 | bytes 8192 | tf_op jit(solution)/shard_map/psum | solution.py:147
  602.7 0.6 subtract_select_fusion.1
  603.4 1.0 copy.69
  (75 shorter events, 4.9 us)
Async XLA Ops:
  7.2 214.7 %copy-start = (bf16[16,512,128]{2,1,0:T(8,128)(2,1)S(1)}, bf16[16,512,128]{2,1,0:T(8,128)(2,1)}, u32[]{:S(2)}) copy-start(bf16[16,512,128]{2,1,0:T(8,128)(2,1)} %param.25) | copy-start | bytes 6291460
  7.2 21.0 %copy-start.4 = (f32[1536]{0:T(1024)S(1)}, f32[1536]{0:T(1024)}, u32[]{:S(2)}) copy-start(f32[1536]{0:T(1024)} %param.18) | copy-start | bytes 18436
  7.2 21.7 %copy-start.6 = (s32[256]{0:T(256)S(1)}, s32[256]{0:T(256)}, u32[]{:S(2)}) copy-start(s32[256]{0:T(256)} %param.23) | copy-start | bytes 3076
  7.2 22.1 %copy-start.7 = (f32[512]{0:T(512)S(1)}, f32[512]{0:T(512)}, u32[]{:S(2)}) copy-start(f32[512]{0:T(512)} %param.19) | copy-start | bytes 6148
  7.2 96.6 %all-gather.5.cloned.1.call-start = ((), (), s32[]{:S(2)}) async-start(), calls=%async_computation.2 | async-start | bytes 1622016 | tf_op jit(solution)/shard_map/all_gather | solution.py:66
  103.8 10.2 %copy-start.9 = (s32[8]{0:T(128)S(1)}, s32[8]{0:T(128)}, u32[]{:S(2)}) copy-start(s32[8]{0:T(128)} %param.22) | copy-start | bytes 100
  107.8 16.4 %all-to-all-start = ((bf16[32,16,288]{2,1,0:T(8,128)(2,1)}), bf16[32,16,288]{2,1,0:T(8,128)(2,1)S(1)}, u32[]{:S(2)}, u32[]{:S(2)}) async-start(bf16[32,16,288]{2,1,0:T(8,128)(2,1)} %bitcast.4), calls=%async_computation | async-start | bytes 786432 | tf_op jit(solution)/shard_map/all_to_all | solution.py:85
  113.9 190.5 %all-gather.7.cloned.1.call-start = ((), (), s32[]{:S(2)}) async-start(), calls=%async_computation.3 | async-start | bytes 2162688 | tf_op jit(solution)/shard_map/all_gather | solution.py:120
  202.6 1.9 copy-start.1
  223.0 225.5 %all-gather.9.cloned.1.call-start = ((), (), s32[]{:S(2)}) async-start(), calls=%async_computation.4 | async-start | bytes 7569408 | tf_op jit(solution)/shard_map/all_gather | solution.py:133
  307.3 48.2 %copy-start.2 = (bf16[7168,16]{0,1:T(8,128)(2,1)S(1)}, bf16[7168,16]{0,1:T(8,128)(2,1)}, u32[]{:S(2)}) copy-start(bf16[7168,16]{0,1:T(8,128)(2,1)} %param.15) | copy-start | bytes 688132
  308.9 46.8 %copy-start.3 = (f32[7168]{0:T(1024)S(1)}, f32[7168]{0:T(1024)}, u32[]{:S(2)}) copy-start(f32[7168]{0:T(1024)} %param.27) | copy-start | bytes 86020
  308.9 47.7 %copy-start.5 = (s32[256]{0:T(256)S(1)}, s32[256]{0:T(256)}, u32[]{:S(2)}) copy-start(s32[256]{0:T(256)} %param.24) | copy-start | bytes 3076
  308.9 47.9 %copy-start.8 = (s32[256,2]{0,1:T(2,128)S(1)}, s32[256,2]{0,1:T(2,128)}, u32[]{:S(2)}) copy-start(s32[256,2]{0,1:T(2,128)} %param.29) | copy-start | bytes 6148
Sparse Core Ops, SparseCore 0:
  29.0 73.0 all-gather.4
  223.1 81.3 all-gather.6
  356.7 91.7 all-gather.8
where the time goes:
time: 618 us; the launch traced here: 611 us
  blocking collectives  250 us (40%)
  waiting for transfers between devices  182 us (29%)
  matrix products  108 us (17%)
  local copies, waits for them, and re-layouts  43.3 us (7%)
  between operations  14.6 us (2%)
  other arithmetic  7.1 us (1%)
  starting transfers between devices  6.22 us (1%)
    all_gather x1, waiting for transfers between devices, on_device(): whole_normed = lax.all_gather(normed, 'dp', axis=1, tiled=True)  90.3 us
    all_gather x1, waiting for transfers between devices, on_device(): lax.all_gather(head_values, 'dp', axis=0, tiled=True)  81.2 us
    pmax x1, blocking collectives, on_device(): vocab_peak = lax.pmax(local_peak, ('dp', 'tp'))  75.1 us
    dot_general x1, matrix products, on_device(): jnp.einsum('usdhc,updc->ushp', arrived, cache_blocks, preferred_element_t...  73.5 us
    psum x1, blocking collectives, on_device(): vocab_total, target = lax.psum((shifted_total, target_part), ('dp', 'tp'))  72.8 us
    all_gather x1, blocking collectives, on_device(): lax.all_gather(fresh_rows, 'dp', axis=0, tiled=True)  40.8 us
    unnamed x24, local copies, waits for them, and re-layouts  36.4 us
    psum x1, blocking collectives, on_device(): block_sum = lax.psum(request_terms, 'tp')  30.8 us
  transfers between devices with their start and end apart: 4, of which 3 were waited for; matrix products, arithmetic and copies ran while one was open for 6% of the time, Pallas kernels for 0%

commit v1 on v0

--- a/solution.py
+++ b/solution.py
@@ -64,7 +64,9 @@
     fresh_rows = jnp.concatenate([latent_part, latent[:, QL + DL :]], axis=1).astype(jnp.bfloat16)
     every_query, every_fresh = (
         lax.all_gather(query_latent, "dp", axis=0, tiled=True),
-        lax.all_gather(fresh_rows, "dp", axis=0, tiled=True),
+        jnp.concatenate(
+            lax.all_to_all(jnp.stack([fresh_rows] * lax.axis_size("dp")), "dp", 0, 0), axis=0
+        ),
     )
     query_part = lax.dot_general(
         every_query, query_weight, (((1,), (2,)), ((), ())), preferred_element_type=jnp.float32

time: 618 us -> 611 us (0.989)
  blocking collectives: 250 us -> 209 us
  waiting for transfers between devices: 182 us -> 205 us
  starting transfers between devices: 6.22 us -> 15.5 us
    all_gather x1 -> x0, blocking collectives: 40.8 us -> none  [on_device(): lax.all_gather(fresh_rows, 'dp', axis=0, tiled=True)]
    all_gather x1, waiting for transfers between devices: 0.02 us -> 29.5 us  [on_device(): lax.all_gather(query_latent, 'dp', axis=0, tiled=True)]
    all_to_all x0 -> x1, starting transfers between devices: none -> 9.84 us  [on_device(): lax.all_to_all(jnp.stack([fresh_rows] * lax.axis_size('dp')), 'dp', 0, 0)]
  transfers between devices with their start and end apart: 4 -> 5, of which waited for: 3 -> 4; matrix products, arithmetic and copies ran while one was open for 6% -> 7% of each run, Pallas kernels for 0% -> 0%
where the time goes in v1:
time: 611 us; the launch traced here: 604 us
  blocking collectives  209 us (34%)
  waiting for transfers between devices  205 us (34%)
  matrix products  107 us (18%)
  local copies, waits for them, and re-layouts  44.9 us (7%)
  starting transfers between devices  15.5 us (3%)
  between operations  14.2 us (2%)
  other arithmetic  7.1 us (1%)
    all_gather x1, waiting for transfers between devices, on_device(): whole_normed = lax.all_gather(normed, 'dp', axis=1, tiled=True)  90.3 us
    all_gather x1, waiting for transfers between devices, on_device(): lax.all_gather(head_values, 'dp', axis=0, tiled=True)  76.2 us
    pmax x1, blocking collectives, on_device(): vocab_peak = lax.pmax(local_peak, ('dp', 'tp'))  75.1 us
    psum x1, blocking collectives, on_device(): vocab_total, target = lax.psum((shifted_total, target_part), ('dp', 'tp'))  72.8 us
    dot_general x1, matrix products, on_device(): jnp.einsum('usdhc,updc->ushp', arrived, cache_blocks, preferred_element_t...  71.6 us
    unnamed x24, local copies, waits for them, and re-layouts  36.4 us
    psum x1, blocking collectives, on_device(): block_sum = lax.psum(request_terms, 'tp')  30.8 us
    all_gather x1, waiting for transfers between devices, on_device(): lax.all_gather(query_latent, 'dp', axis=0, tiled=True)  29.5 us
  transfers between devices with their start and end apart: 5, of which 4 were waited for; matrix products, arithmetic and copies ran while one was open for 7% of the time, Pallas kernels for 0%

profile of v1, /device:TPU:1, one launch (start us, length us, event | category | flops | bytes accessed | tf_op | source)
XLA Modules:
  0.0 603.9 jit_solution(6321121302445125948)
XLA Ops:
  7.3 1.2 fusion.38
  8.5 3.4 convolution_bitcast_fusion.1
  11.9 15.8 %all-gather = f32[8,264,16]{1,2,0:T(8,128)S(1)} all-gather(f32[1,264,16]{1,2,0:T(8,128)S(1)} %convolution_bitcast_fusion.1), channel_id=1, replica_groups=mesh['dp'=32,'tp'=8] {'tp'}, dimensions={0}, use_global_device_ids=true | all-gather | bytes 152064 | tf_op jit(solution)/shard_map/all_gather | solution.py:59
  28.2 0.7 multiply_convert_fusion
  29.1 0.9 stack.2
  30.0 9.8 %all-to-all-start.1 = ((bf16[32,16,576]{2,1,0:T(8,128)(2,1)}), bf16[32,16,576]{2,1,0:T(8,128)(2,1)S(1)}, u32[]{:S(2)}, u32[]{:S(2)}) async-start(bf16[32,16,576]{2,1,0:T(8,128)(2,1)} %stack.2), calls=%async_computation.1 | async-start | bytes 1310720 | tf_op jit(solution)/shard_map/all_to_all | solution.py:68
  40.2 32.8 %copy.58 = bf16[8,4096,576]{1,0,2:T(8,128)(2,1)} copy(bf16[8,4096,576]{1,2,0:T(8,128)(2,1)} %param.21) | data formatting | bytes 75497472 | tf_op args[6]
  73.0 29.5 %all-gather.5.cloned.1.call-done = bf16[512,1536]{1,0:T(8,128)(2,1)} async-done(((bf16[16,1536]{1,0:T(8,128)(2,1)}), bf16[512,1536]{1,0:T(8,128)(2,1)}) %all-gather.5.cloned.1.call-update) | async-done | bytes 1572880 | tf_op jit(solution)/shard_map/all_gather | solution.py:66
  102.5 2.6 fusion.19
  105.1 0.8 reshape.222
  105.9 1.3 convolution_convert_fusion
  107.2 0.9 copy.56
  108.1 5.6 all-to-all-start
  114.7 9.3 %all-to-all-done = bf16[32,16,288]{2,1,0:T(8,128)(2,1)S(1)} async-done(((bf16[32,16,288]{2,1,0:T(8,128)(2,1)}), bf16[32,16,288]{2,1,0:T(8,128)(2,1)S(1)}, u32[]{:S(2)}, u32[]{:S(2)}) %all-to-all-start) | async-done | bytes 294944 | tf_op jit(solution)/shard_map/all_to_all | solution.py:87
  124.0 2.2 copy.57
  126.2 2.8 fusion.50
  128.9 71.6 %fusion.8 = (f32[8,2,16]{2,1,0:T(2,128)S(1)}, f32[8,2,16,4096]{3,2,1,0:T(8,128)S(1)}) fusion(pred[8,4096]{1,0:T(8,128)(4,1)S(1)} %iota_compare_fusion.2, bf16[8,4096,32,18,1]{1,0,3,2,4:T(8,128)(2,1)} %bitcast.78, bf16[8,2,32,16,18]{2,1,0,4,3:T(2,128)(2,1)} %bitcast.82), kind=kOutput, calls=%fused_computation.10 | convolution fusion | flops 1211105024 | bytes 42271744 | tf_op jit(solution)/shard_map/usdhc,updc->ushp/dot_general | solution.py:92
  200.7 1.9 copy-done.1
  202.5 1.2 fusion.9
  203.7 15.8 %fusion.2 = f32[8,2,16,512]{3,2,1,0:T(8,128)S(1)} fusion(bf16[8,4096,576]{1,2,0:T(8,128)(2,1)} %param.21, f32[8,2,16,4096]{3,2,1,0:T(8,128)} %copy-done.1, f32[8,2,16]{2,1,0:T(2,128)S(1)} %add.129, f32[8,2,16]{2,1,0:T(2,128)S(1)} %max.9, pred[8,4096]{1,0:T(8,128)(4,1)S(1)} %iota_compare_fusion.2), kind=kOutput, calls=%fused_computation.3 | convolution fusion | flops 1078984704 | bytes 38307840 | tf_op jit(solution)/shard_map/ushp,upc->ushc/dot_general | solution.py:109
  221.2 76.2 %all-gather.7.cloned.1.call-done = bf16[512,2048]{1,0:T(8,128)(2,1)} async-done(((bf16[16,2048]{1,0:T(8,128)(2,1)}), bf16[512,2048]{1,0:T(8,128)(2,1)}) %all-gather.7.cloned.1.call-update) | async-done | bytes 2097168 | tf_op jit(solution)/shard_map/all_gather | solution.py:122
  297.5 2.6 convolution_bitcast_fusion
  300.3 1.6 gather_fusion
  302.1 30.8 %all-reduce.2 = bf16[224,512]{0,1:T(8,128)(2,1)S(1)} all-reduce(f32[224,512]{0,1:T(8,128)S(1)} %select_bitcast_fusion), channel_id=1, replica_groups=mesh['dp'=32,'tp'=8] {'tp'}, use_global_device_ids=true, to_apply=%region_7.8 | all-reduce | flops 114688 | bytes 688128 | tf_op jit(solution)/shard_map/psum | solution.py:127
  332.9 14.9 %all_to_all.34 = bf16[224,32,16]{0,2,1:T(8,128)(2,1)S(1)} all-to-all(bf16[224,32,16]{0,2,1:T(8,128)(2,1)S(1)} %bitcast.83), channel_id=1, replica_groups=mesh['dp'=32,'tp'=8] {'dp'}, dimensions={1} | all-to-all | bytes 458752 | tf_op jit(solution)/shard_map/all_to_all | solution.py:128
  348.7 0.8 fusion.36
  350.4 0.7 broadcast_select_fusion
  351.1 90.3 %all-gather.9.cloned.1.call-done = bf16[7168,512]{0,1:T(8,128)(2,1)} async-done(((bf16[7168,16]{0,1:T(8,128)(2,1)}), bf16[7168,512]{0,1:T(8,128)(2,1)}) %all-gather.9.cloned.1.call-update) | async-done | bytes 7340048 | tf_op jit(solution)/shard_map/all_gather | solution.py:135
  441.5 6.2 %fusion.51 = (f32[512]{0:T(512)S(1)}, f32[512,256]{0,1:T(8,128)S(1)}) fusion(bf16[7168,512]{0,1:T(8,128)(2,1)} %all-gather.9.cloned.1.call-done, bf16[7168,256]{1,0:T(8,128)(2,1)} %param.28), kind=kOutput, calls=%fused_computation.95 | convolution fusion | flops 1879178752 | bytes 11536384 | tf_op jit(solution)/shard_map/dot_general | solution.py:136
  447.7 75.1 %pmax.7 = f32[512]{0:T(512)S(1)} all-reduce(f32[512]{0:T(512)S(1)} %get-tuple-element.25), channel_id=1, replica_groups=mesh['dp'=32,'tp'=8] {'dp','tp'}, use_global_device_ids=true, to_apply=%region_10.11 | all-reduce | flops 512 | bytes 4096 | tf_op jit(solution)/shard_map/pmax | solution.py:147
  522.9 72.8 %all-reduce = (f32[512]{0:T(512)S(1)}, f32[512]{0:T(512)S(1)}) all-reduce(f32[512]{0:T(512)S(1)} %get-tuple-element.16, f32[512]{0:T(512)S(1)} %get-tuple-element.15), channel_id=1, replica_groups=mesh['dp'=32,'tp'=8] {'dp','tp'}, use_global_device_ids=true, to_apply=%region_12.13 | all-reduce | flops 1024 | bytes 8192 | tf_op jit(solution)/shard_map/psum | solution.py:149
  596.4 1.0 copy.69
  (77 shorter events, 6.5 us)
Async XLA Ops:
  7.2 212.7 %copy-start = (bf16[16,512,128]{2,1,0:T(8,128)(2,1)S(1)}, bf16[16,512,128]{2,1,0:T(8,128)(2,1)}, u32[]{:S(2)}) copy-start(bf16[16,512,128]{2,1,0:T(8,128)(2,1)} %param.25) | copy-start | bytes 6291460
  7.2 21.0 %copy-start.4 = (f32[1536]{0:T(1024)S(1)}, f32[1536]{0:T(1024)}, u32[]{:S(2)}) copy-start(f32[1536]{0:T(1024)} %param.18) | copy-start | bytes 18436
  7.2 21.8 %copy-start.7 = (f32[512]{0:T(512)S(1)}, f32[512]{0:T(512)}, u32[]{:S(2)}) copy-start(f32[512]{0:T(512)} %param.19) | copy-start | bytes 6148
  7.2 32.6 %copy-start.9 = (s32[8]{0:T(128)S(1)}, s32[8]{0:T(128)}, u32[]{:S(2)}) copy-start(s32[8]{0:T(128)} %param.22) | copy-start | bytes 100
  7.2 32.7 %copy-start.6 = (s32[256]{0:T(256)S(1)}, s32[256]{0:T(256)}, u32[]{:S(2)}) copy-start(s32[256]{0:T(256)} %param.23) | copy-start | bytes 3076
  7.2 95.3 %all-gather.5.cloned.1.call-start = ((), (), s32[]{:S(2)}) async-start(), calls=%async_computation.3 | async-start | bytes 1622016 | tf_op jit(solution)/shard_map/all_gather | solution.py:66
  30.0 78.1 %all-to-all-start.1 = ((bf16[32,16,576]{2,1,0:T(8,128)(2,1)}), bf16[32,16,576]{2,1,0:T(8,128)(2,1)S(1)}, u32[]{:S(2)}, u32[]{:S(2)}) async-start(bf16[32,16,576]{2,1,0:T(8,128)(2,1)} %stack.2), calls=%async_computation.1 | async-start | bytes 1310720 | tf_op jit(solution)/shard_map/all_to_all | solution.py:68
  108.1 15.8 %all-to-all-start = ((bf16[32,16,288]{2,1,0:T(8,128)(2,1)}), bf16[32,16,288]{2,1,0:T(8,128)(2,1)S(1)}, u32[]{:S(2)}, u32[]{:S(2)}) async-start(bf16[32,16,288]{2,1,0:T(8,128)(2,1)} %bitcast.4), calls=%async_computation | async-start | bytes 786432 | tf_op jit(solution)/shard_map/all_to_all | solution.py:87
  113.7 183.8 %all-gather.7.cloned.1.call-start = ((), (), s32[]{:S(2)}) async-start(), calls=%async_computation.4 | async-start | bytes 2162688 | tf_op jit(solution)/shard_map/all_gather | solution.py:122
  200.6 1.9 copy-start.1
  221.0 220.5 %all-gather.9.cloned.1.call-start = ((), (), s32[]{:S(2)}) async-start(), calls=%async_computation.5 | async-start | bytes 7569408 | tf_op jit(solution)/shard_map/all_gather | solution.py:135
  300.3 48.2 %copy-start.2 = (bf16[7168,16]{0,1:T(8,128)(2,1)S(1)}, bf16[7168,16]{0,1:T(8,128)(2,1)}, u32[]{:S(2)}) copy-start(bf16[7168,16]{0,1:T(8,128)(2,1)} %param.15) | copy-start | bytes 688132
  301.9 46.8 %copy-start.3 = (f32[7168]{0:T(1024)S(1)}, f32[7168]{0:T(1024)}, u32[]{:S(2)}) copy-start(f32[7168]{0:T(1024)} %param.27) | copy-start | bytes 86020
  301.9 47.7 %copy-start.5 = (s32[256]{0:T(256)S(1)}, s32[256]{0:T(256)}, u32[]{:S(2)}) copy-start(s32[256]{0:T(256)} %param.24) | copy-start | bytes 3076
  301.9 47.9 %copy-start.8 = (s32[256,2]{0,1:T(2,128)S(1)}, s32[256,2]{0,1:T(2,128)}, u32[]{:S(2)}) copy-start(s32[256,2]{0,1:T(2,128)} %param.29) | copy-start | bytes 6148
Sparse Core Ops, SparseCore 0:
  29.0 73.4 all-gather.4
  221.1 76.3 all-gather.6
  349.7 91.7 all-gather.8
